TPU v7x, 32 devices: a whole 2x2x4 slice. The times are simulated.
32 devices in a mesh: row: 4 (over y, x), col: 8 (over z, core).
Axes of the slice: x: 2, y: 2, z: 4, core: 2. Of those that a mesh axis runs over, the one named last changes fastest.
Arguments:
- pair_window: bfloat16 [8, 16, 32, 128], P('col', 'row'), may hold values from -6 to 6
- tri_cotangent: bfloat16 [8, 16, 128, 128], P(None, 'row', 'col'), may hold values from -0.75 to 0.75
- saved_left: bfloat16 [8, 16, 32, 128], P('col', 'row'), may hold values from -6 to 6
- saved_right: bfloat16 [8, 16, 32, 128], P('col', 'row'), may hold values from -6 to 6
- norm_gain: float32 [128], replicated, may hold values from 0.5 to 1.5
- norm_bias: float32 [128], replicated, may hold values from -3 to 3
- proj_weight: bfloat16 [4, 128, 128], replicated, may hold values from -0.5 to 0.5
Outputs:
- pair_grad: bfloat16 [8, 16, 32, 128], P('col', 'row')
- weight_grad: float32 [4, 128, 128], replicated
- norm_grad: float32 [2, 128], replicated
All inputs are finite; a program needn't handle non-finite values.
Results may differ from a plain program's by a relative error of at most 0.0085.
Values may be sent and summed in bfloat16 or wider, within the bound.
A program may use at most 64 MiB of HBM per device.

v0:
```python
import jax
import jax.numpy as jnp
from jax import lax
from jax.sharding import PartitionSpec as P


def gated_norm_back(pair_rows, left_grad, right_grad, norm_gain, norm_bias, proj_weight):
    pair = pair_rows.astype(jnp.float32)
    average = jnp.mean(pair, axis=-1, keepdims=True)
    centred = pair - average
    variance = jnp.mean(centred * centred, axis=-1, keepdims=True)
    inv_std = lax.rsqrt(variance + 1e-05)
    unit_pair = centred * inv_std
    normed = (unit_pair * norm_gain + norm_bias).astype(jnp.bfloat16)
    chans = proj_weight.shape[2]
    stacked = jnp.transpose(proj_weight, (1, 0, 2)).reshape(proj_weight.shape[1], 4 * chans)
    preact = jnp.dot(normed, stacked, preferred_element_type=jnp.float32)
    gate_left = jax.nn.sigmoid(preact[:, :chans])
    value_left = preact[:, chans : 2 * chans]
    gate_right = jax.nn.sigmoid(preact[:, 2 * chans : 3 * chans])
    value_right = preact[:, 3 * chans :]
    pre_grads = jnp.concatenate(
        [
            left_grad * value_left * gate_left * (1.0 - gate_left),
            left_grad * gate_left,
            right_grad * value_right * gate_right * (1.0 - gate_right),
            right_grad * gate_right,
        ],
        axis=1,
    ).astype(jnp.bfloat16)
    weight_part = lax.dot_general(
        normed, pre_grads, (((0,), (0,)), ((), ())), preferred_element_type=jnp.float32
    )
    weight_part = jnp.transpose(weight_part.reshape(proj_weight.shape[1], 4, chans), (1, 0, 2))
    normed_grad = jnp.dot(pre_grads, stacked.T, preferred_element_type=jnp.float32)
    norm_part = jnp.stack([jnp.sum(normed_grad * unit_pair, axis=0), jnp.sum(normed_grad, axis=0)])
    scaled_grad = normed_grad * norm_gain
    pair_grad = inv_std * (
        scaled_grad
        - jnp.mean(scaled_grad, axis=-1, keepdims=True)
        - unit_pair * jnp.mean(scaled_grad * unit_pair, axis=-1, keepdims=True)
    )
    return (pair_grad.astype(jnp.bfloat16), weight_part, norm_part)


def on_device(
    pair_window, tri_cotangent, saved_left, saved_right, norm_gain, norm_bias, proj_weight
):
    block_count, own_rows, col_tokens, channels = tri_cotangent.shape
    window_len = saved_left.shape[2]
    right_rows = lax.all_gather(saved_right, "row", axis=1, tiled=True)[0]
    cot_flat = tri_cotangent.reshape(block_count * own_rows, col_tokens, channels)
    cot_piece = cot_flat
    left_grad = lax.psum_scatter(
        jnp.einsum("ijh,jkh->ikh", cot_piece, right_rows, preferred_element_type=jnp.float32),
        "col",
        scatter_dimension=0,
        tiled=True,
    )
    left_rows = lax.all_gather(saved_left, "col", axis=0, tiled=True)
    left_flat = left_rows.reshape(block_count * own_rows, window_len, channels)
    cot_piece = cot_flat
    right_grad = lax.psum_scatter(
        jnp.einsum("ijh,ikh->jkh", cot_piece, left_flat, preferred_element_type=jnp.float32),
        "row",
        scatter_dimension=0,
        tiled=True,
    )
    positions = own_rows * window_len
    pair_grad, weight_part, norm_part = gated_norm_back(
        pair_window.reshape(positions, pair_window.shape[3]),
        left_grad.reshape(positions, channels),
        right_grad.reshape(positions, channels),
        norm_gain,
        norm_bias,
        proj_weight,
    )
    weight_grad, norm_grad = lax.psum((weight_part, norm_part), ("row", "col"))
    return (pair_grad.reshape(pair_window.shape), weight_grad, norm_grad)


def solution(mesh):
    return jax.shard_map(
        on_device,
        mesh=mesh,
        in_specs=(
            P("col", "row", None, None),
            P(None, "row", "col", None),
            P("col", "row", None, None),
            P("col", "row", None, None),
            P(),
            P(),
            P(),
        ),
        out_specs=(P("col", "row", None, None), P(), P()),
        check_vma=False,
    )
```

profile of v0, /device:TPU:0, one launch (start us, length us, event | category | flops | bytes accessed | tf_op | source)
XLA Modules:
  0.0 225.6 jit_solution(12033966803922568109)
XLA Ops:
  7.2 0.0 reduce-scatter.5.cloned.1.call-start
  7.2 1.4 copy.28
  8.6 16.1 %all_gather.7 = bf16[8,4,32,128]{3,2,1,0:T(8,128)(2,1)S(1)} all-gather(bf16[1,4,32,128]{3,2,1,0:T(8,128)(2,1)} %param.9), channel_id=1, replica_groups=mesh['row'=4,'col'=8] {'col'}, dimensions={0}, use_global_device_ids=true | all-gather | bytes 294912 | tf_op jit(solution)/shard_map/all_gather | solution.py:60
  24.8 0.9 copy.31
  25.7 0.4 convolution_bitcast_fusion.1
  26.1 1.1 copy.33
  27.2 0.0 reduce-scatter.5.cloned.1.call-update
  27.3 0.0 reduce-scatter.3.cloned.1.call-start
  27.3 8.5 %all_gather.6 = bf16[1,16,32,128]{3,2,0,1:T(8,128)(2,1)S(1)} all-gather(bf16[1,4,32,128]{3,2,0,1:T(8,128)(2,1)S(1)} %bitcast.59), channel_id=1, replica_groups=mesh['row'=4,'col'=8] {'row'}, dimensions={1}, use_global_device_ids=true | all-gather | bytes 163840 | tf_op jit(solution)/shard_map/all_gather | solution.py:51
  35.8 0.4 copy.27
  36.2 0.5 convolution_bitcast_fusion
  36.8 2.2 copy.29
  39.0 0.0 reduce-scatter.3.cloned.1.call-update
  39.0 0.0 all-reduce.2.cloned.1.call-start
  39.1 0.1 convert_reduce_fusion
  39.2 0.1 div.25
  39.3 0.2 multiply_reduce_fusion.2
  39.5 0.1 rsqrt.13
  39.6 0.1 copy.30
  39.7 0.1 add_convert_fusion
  39.8 0.2 fusion.19
  40.0 12.8 %reduce-scatter.5.cloned.1.call-done = f32[4,32,128]{2,1,0:T(8,128)} async-done(((f32[16,32,128]{2,1,0:T(8,128)}), f32[4,32,128]{2,1,0:T(8,128)}) %reduce-scatter.5.cloned.1.call-update) | async-done | bytes 65552 | tf_op jit(solution)/shard_map/reduce_scatter | solution.py:63
  52.8 33.6 %reduce-scatter.3.cloned.1.call-done = f32[4,32,128]{2,1,0:T(8,128)} async-done(((f32[32,32,128]{2,1,0:T(8,128)}), f32[4,32,128]{2,1,0:T(8,128)}) %reduce-scatter.3.cloned.1.call-update) | async-done | bytes 65552 | tf_op jit(solution)/shard_map/reduce_scatter | solution.py:54
  86.4 0.9 fusion.12
  87.4 0.1 copy.38
  87.5 0.9 convolution_bitcast_fusion.2
  88.4 0.0 all-reduce.2.cloned.1.call-update
  88.4 0.3 multiply_reduce_fusion
  88.7 37.9 %psum.15 = f32[2,128]{1,0:T(2,128)} all-reduce(f32[2,128]{1,0:T(2,128)S(1)} %pad_maximum_fusion.2), channel_id=1, replica_groups=mesh['row'=4,'col'=8] {'row','col'}, use_global_device_ids=true, to_apply=%region_9.0 | all-reduce | flops 256 | bytes 2048 | tf_op jit(solution)/shard_map/psum | solution.py:78
  126.6 0.8 multiply_convert_fusion
  127.4 90.0 %all-reduce.2.cloned.1.call-done = f32[4,128,128]{2,1,0:T(8,128)} async-done(((f32[4,128,128]{2,1,0:T(8,128)}), f32[4,128,128]{2,1,0:T(8,128)}) %all-reduce.2.cloned.1.call-update) | async-done | bytes 262160 | tf_op jit(solution)/shard_map/psum | solution.py:78
  217.5 1.7 copy.40
  (15 shorter events, 0.1 us)
Async XLA Ops:
  7.2 45.6 %reduce-scatter.5.cloned.1.call-start = ((), (), s32[]{:S(2)}) async-start(), calls=%async_computation.3 | async-start | bytes 327680 | tf_op jit(solution)/shard_map/reduce_scatter | solution.py:63
  25.7 1.6 copy-start.2
  27.3 59.1 %reduce-scatter.3.cloned.1.call-start = ((), (), s32[]{:S(2)}) async-start(), calls=%async_computation.2 | async-start | bytes 589824 | tf_op jit(solution)/shard_map/reduce_scatter | solution.py:54
  36.8 2.3 %copy-start = (bf16[1,4,32,128]{3,2,1,0:T(8,128)(2,1)S(1)}, bf16[1,4,32,128]{3,2,1,0:T(8,128)(2,1)}, u32[]{:S(2)}) copy-start(bf16[1,4,32,128]{3,2,1,0:T(8,128)(2,1)} %param.7) | copy-start | bytes 98308
  36.8 2.8 %copy-start.1 = (bf16[4,128,128]{2,1,0:T(8,128)(2,1)S(1)}, bf16[4,128,128]{2,1,0:T(8,128)(2,1)}, u32[]{:S(2)}) copy-start(bf16[4,128,128]{2,1,0:T(8,128)(2,1)} %param.13) | copy-start | bytes 393220
  36.8 2.9 %copy-start.3 = (f32[128]{0:T(128)S(1)}, f32[128]{0:T(128)}, u32[]{:S(2)}) copy-start(f32[128]{0:T(128)} %param.11) | copy-start | bytes 1540
  36.8 2.9 %copy-start.4 = (f32[128]{0:T(128)S(1)}, f32[128]{0:T(128)}, u32[]{:S(2)}) copy-start(f32[128]{0:T(128)} %param.12) | copy-start | bytes 1540
  39.0 178.4 %all-reduce.2.cloned.1.call-start = ((), (), s32[]{:S(2)}) async-start(), calls=%async_computation.4 | async-start | bytes 524288 | tf_op jit(solution)/shard_map/psum | solution.py:78
Sparse Core Ops, SparseCore 0:
  27.4 25.3 reduce-scatter.4
  55.0 31.3 reduce-scatter.2
  92.5 124.9 all-reduce.1
where the time goes:
time: 226 us
  waiting for transfers between devices  136 us (60%)
  blocking collectives  62.5 us (28%)
  between operations  13.9 us (6%)
  local copies, waits for them, and re-layouts  8.23 us (4%)
  matrix products  2.3 us (1%)
    psum x1, waiting for transfers between devices, on_device(): weight_grad, norm_grad = lax.psum((weight_part, norm_part), ('row', 'col'))  90 us
    psum x1, blocking collectives, on_device(): weight_grad, norm_grad = lax.psum((weight_part, norm_part), ('row', 'col'))  37.9 us
    reduce_scatter x1, waiting for transfers between devices, on_device(): lax.psum_scatter(jnp.einsum('ijh,jkh->ikh', cot_piece, right_rows, prefer...  33.6 us
    all_gather x1, blocking collectives, on_device(): left_rows = lax.all_gather(saved_left, 'col', axis=0, tiled=True)  16.1 us
    reduce_scatter x1, waiting for transfers between devices, on_device(): lax.psum_scatter(jnp.einsum('ijh,ikh->jkh', cot_piece, left_flat, preferr...  12.8 us
    all_gather x1, blocking collectives, on_device(): right_rows = lax.all_gather(saved_right, 'row', axis=1, tiled=True)[0]  8.46 us
  transfers between devices with their start and end apart: 3, of which 3 were waited for; matrix products, arithmetic and copies ran while one was open for 2% of the time, Pallas kernels for 0%

commit v1 on v0

--- a/solution.py
+++ b/solution.py
@@ -57,7 +57,12 @@
         scatter_dimension=0,
         tiled=True,
     )
-    left_rows = lax.all_gather(saved_left, "col", axis=0, tiled=True)
+    ring = [saved_left]
+    for hop in range(7):
+        ring.append(lax.ppermute(ring[-1], "col", [(dev, (dev + 1) % 8) for dev in range(8)]))
+    left_rows = jnp.roll(
+        jnp.concatenate(ring[::-1], axis=0), (lax.axis_index("col") + 1) * ring[0].shape[0], axis=0
+    )
     left_flat = left_rows.reshape(block_count * own_rows, window_len, channels)
     cot_piece = cot_flat
     right_grad = lax.psum_scatter(

time: 226 us -> 245 us (1.084)
  waiting for transfers between devices: 136 us -> 169 us
  blocking collectives: 62.5 us -> 46.8 us
    ppermute x0 -> x7, waiting for transfers between devices: none -> 35.2 us  [on_device(): lax.ppermute(ring[-1], 'col', [(dev, (dev + 1) % 8) for dev in range(8)])]
    all_gather x1 -> x0, blocking collectives: 16.1 us -> none  [on_device(): left_rows = lax.all_gather(saved_left, 'col', axis=0, tiled=True)]
    reduce_scatter x1, waiting for transfers between devices: 12.8 us -> 9.97 us  [on_device(): lax.psum_scatter(jnp.einsum('ijh,ikh->jkh', cot_piece, left_flat, preferr...]
  transfers between devices with their start and end apart: 3 -> 10, of which waited for: 3 -> 10; matrix products, arithmetic and copies ran while one was open for 2% -> 3% of each run, Pallas kernels for 0% -> 0%
where the time goes in v1:
time: 245 us
  waiting for transfers between devices  169 us (69%)
  blocking collectives  46.8 us (19%)
  between operations  14 us (6%)
  local copies, waits for them, and re-layouts  9.93 us (4%)
    psum x1, waiting for transfers between devices, on_device(): weight_grad, norm_grad = lax.psum((weight_part, norm_part), ('row', 'col'))  90.1 us
    psum x1, blocking collectives, on_device(): weight_grad, norm_grad = lax.psum((weight_part, norm_part), ('row', 'col'))  37.9 us
    ppermute x7, waiting for transfers between devices, on_device(): lax.ppermute(ring[-1], 'col', [(dev, (dev + 1) % 8) for dev in range(8)])  35.2 us
    reduce_scatter x1, waiting for transfers between devices, on_device(): lax.psum_scatter(jnp.einsum('ijh,jkh->ikh', cot_piece, right_rows, prefer...  33.7 us
    reduce_scatter x1, waiting for transfers between devices, on_device(): lax.psum_scatter(jnp.einsum('ijh,ikh->jkh', cot_piece, left_flat, preferr...  9.97 us
    all_gather x1, blocking collectives, on_device(): right_rows = lax.all_gather(saved_right, 'row', axis=1, tiled=True)[0]  8.96 us
  transfers between devices with their start and end apart: 10, of which 10 were waited for; matrix products, arithmetic and copies ran while one was open for 3% of the time, Pallas kernels for 0%

profile of v1, /device:TPU:0, one launch (start us, length us, event | category | flops | bytes accessed | tf_op | source)
XLA Modules:
  0.0 244.8 jit_solution(9997703829220792245)
XLA Ops:
  7.2 0.5 collective-permute-start
  7.8 5.8 %collective-permute-done = bf16[1,4,32,128]{3,2,1,0:T(8,128)(2,1)S(1)} collective-permute-done((bf16[1,4,32,128]{3,2,1,0:T(8,128)(2,1)}, bf16[1,4,32,128]{3,2,1,0:T(8,128)(2,1)S(1)}, u32[]{:S(2)}, u32[]{:S(2)}) %collective-permute-start) | collective-permute-done | bytes 32800 | tf_op jit(solution)/shard_map/ppermute | solution.py:62
  13.6 5.1 %collective-permute-done.1 = bf16[1,4,32,128]{3,2,1,0:T(8,128)(2,1)S(1)} collective-permute-done((bf16[1,4,32,128]{3,2,1,0:T(8,128)(2,1)S(1)}, bf16[1,4,32,128]{3,2,1,0:T(8,128)(2,1)S(1)}, u32[]{:S(2)}, u32[]{:S(2)}) %collective-permute-start.1) | collective-permute-done | bytes 32800 | tf_op jit(solution)/shard_map/ppermute | solution.py:62
  18.7 5.1 %collective-permute-done.2 = bf16[1,4,32,128]{3,2,1,0:T(8,128)(2,1)S(1)} collective-permute-done((bf16[1,4,32,128]{3,2,1,0:T(8,128)(2,1)S(1)}, bf16[1,4,32,128]{3,2,1,0:T(8,128)(2,1)S(1)}, u32[]{:S(2)}, u32[]{:S(2)}) %collective-permute-start.2) | collective-permute-done | bytes 32800 | tf_op jit(solution)/shard_map/ppermute | solution.py:62
  23.9 5.1 %collective-permute-done.3 = bf16[1,4,32,128]{3,2,1,0:T(8,128)(2,1)S(1)} collective-permute-done((bf16[1,4,32,128]{3,2,1,0:T(8,128)(2,1)S(1)}, bf16[1,4,32,128]{3,2,1,0:T(8,128)(2,1)S(1)}, u32[]{:S(2)}, u32[]{:S(2)}) %collective-permute-start.3) | collective-permute-done | bytes 32800 | tf_op jit(solution)/shard_map/ppermute | solution.py:62
  29.0 5.1 %collective-permute-done.4 = bf16[1,4,32,128]{3,2,1,0:T(8,128)(2,1)S(1)} collective-permute-done((bf16[1,4,32,128]{3,2,1,0:T(8,128)(2,1)S(1)}, bf16[1,4,32,128]{3,2,1,0:T(8,128)(2,1)S(1)}, u32[]{:S(2)}, u32[]{:S(2)}) %collective-permute-start.4) | collective-permute-done | bytes 32800 | tf_op jit(solution)/shard_map/ppermute | solution.py:62
  34.1 5.1 %collective-permute-done.5 = bf16[1,4,32,128]{3,2,1,0:T(8,128)(2,1)S(1)} collective-permute-done((bf16[1,4,32,128]{3,2,1,0:T(8,128)(2,1)S(1)}, bf16[1,4,32,128]{3,2,1,0:T(8,128)(2,1)S(1)}, u32[]{:S(2)}, u32[]{:S(2)}) %collective-permute-start.5) | collective-permute-done | bytes 32800 | tf_op jit(solution)/shard_map/ppermute | solution.py:62
  39.3 1.4 copy.28
  40.7 3.7 %collective-permute-done.6 = bf16[1,4,32,128]{3,2,1,0:T(8,128)(2,1)S(1)} collective-permute-done((bf16[1,4,32,128]{3,2,1,0:T(8,128)(2,1)S(1)}, bf16[1,4,32,128]{3,2,1,0:T(8,128)(2,1)S(1)}, u32[]{:S(2)}, u32[]{:S(2)}) %collective-permute-start.6) | collective-permute-done | bytes 32800 | tf_op jit(solution)/shard_map/ppermute | solution.py:62
  44.5 0.8 constant_dynamic-update-slice_fusion.8
  45.4 0.8 constant_dynamic-update-slice_fusion
  46.2 0.9 copy.31
  47.1 0.4 convolution_bitcast_fusion.1
  47.5 1.1 copy.33
  48.7 9.0 %all_gather.3 = bf16[1,16,32,128]{3,2,0,1:T(8,128)(2,1)S(1)} all-gather(bf16[1,4,32,128]{3,2,0,1:T(8,128)(2,1)S(1)} %bitcast.59), channel_id=1, replica_groups=mesh['row'=4,'col'=8] {'row'}, dimensions={1}, use_global_device_ids=true | all-gather | bytes 163840 | tf_op jit(solution)/shard_map/all_gather | solution.py:51
  57.7 0.4 copy.27
  58.1 0.5 convolution_bitcast_fusion
  58.7 2.2 copy.29
  61.2 0.2 multiply_reduce_fusion.2
  61.5 0.1 copy.30
  61.6 0.1 add_convert_fusion
  61.7 0.2 fusion.19
  61.9 10.0 %reduce-scatter.5.cloned.1.call-done = f32[4,32,128]{2,1,0:T(8,128)} async-done(((f32[16,32,128]{2,1,0:T(8,128)}), f32[4,32,128]{2,1,0:T(8,128)}) %reduce-scatter.5.cloned.1.call-update) | async-done | bytes 65552 | tf_op jit(solution)/shard_map/reduce_scatter | solution.py:68
  71.9 33.7 %reduce-scatter.3.cloned.1.call-done = f32[4,32,128]{2,1,0:T(8,128)} async-done(((f32[32,32,128]{2,1,0:T(8,128)}), f32[4,32,128]{2,1,0:T(8,128)}) %reduce-scatter.3.cloned.1.call-update) | async-done | bytes 65552 | tf_op jit(solution)/shard_map/reduce_scatter | solution.py:54
  105.6 0.9 fusion.12
  106.5 0.1 copy.38
  106.7 0.9 convolution_bitcast_fusion.2
  107.6 0.3 multiply_reduce_fusion
  107.9 37.9 %psum.15 = f32[2,128]{1,0:T(2,128)} all-reduce(f32[2,128]{1,0:T(2,128)S(1)} %pad_maximum_fusion.2), channel_id=1, replica_groups=mesh['row'=4,'col'=8] {'row','col'}, use_global_device_ids=true, to_apply=%region_9.10 | all-reduce | flops 256 | bytes 2048 | tf_op jit(solution)/shard_map/psum | solution.py:83
  145.8 0.8 multiply_convert_fusion
  146.5 90.1 %all-reduce.2.cloned.1.call-done = f32[4,128,128]{2,1,0:T(8,128)} async-done(((f32[4,128,128]{2,1,0:T(8,128)}), f32[4,128,128]{2,1,0:T(8,128)}) %all-reduce.2.cloned.1.call-update) | async-done | bytes 262160 | tf_op jit(solution)/shard_map/psum | solution.py:83
  236.6 1.7 copy.55
  (45 shorter events, 0.7 us)
Async XLA Ops:
  7.2 64.7 %reduce-scatter.5.cloned.1.call-start = ((), (), s32[]{:S(2)}) async-start(), calls=%async_computation.3 | async-start | bytes 327680 | tf_op jit(solution)/shard_map/reduce_scatter | solution.py:68
  7.2 6.4 %collective-permute-start = (bf16[1,4,32,128]{3,2,1,0:T(8,128)(2,1)}, bf16[1,4,32,128]{3,2,1,0:T(8,128)(2,1)S(1)}, u32[]{:S(2)}, u32[]{:S(2)}) collective-permute-start(bf16[1,4,32,128]{3,2,1,0:T(8,128)(2,1)} %param.9), channel_id=1, source_target_pairs={{0,1},{1,2},{2,3},{3,4},{4,5},{5,6},{6,7},{7,0},{8,9},{9,10},{10,1... | collective-permute-start | bytes 98312 | tf_op jit(solution)/shard_map/ppermute | solution.py:62
  13.6 5.1 %collective-permute-start.1 = (bf16[1,4,32,128]{3,2,1,0:T(8,128)(2,1)S(1)}, bf16[1,4,32,128]{3,2,1,0:T(8,128)(2,1)S(1)}, u32[]{:S(2)}, u32[]{:S(2)}) collective-permute-start(bf16[1,4,32,128]{3,2,1,0:T(8,128)(2,1)S(1)} %collective-permute-done), channel_id=1, source_target_pairs={{0,1},{1,2},{2,3},{3,4},{4,5},{5,6},{6,7},{7,0},{8,9},{9,10},{10,1... | collective-permute-start | bytes 98312 | tf_op jit(solution)/shard_map/ppermute | solution.py:62
  18.7 5.1 %collective-permute-start.2 = (bf16[1,4,32,128]{3,2,1,0:T(8,128)(2,1)S(1)}, bf16[1,4,32,128]{3,2,1,0:T(8,128)(2,1)S(1)}, u32[]{:S(2)}, u32[]{:S(2)}) collective-permute-start(bf16[1,4,32,128]{3,2,1,0:T(8,128)(2,1)S(1)} %collective-permute-done.1), channel_id=1, source_target_pairs={{0,1},{1,2},{2,3},{3,4},{4,5},{5,6},{6,7},{7,0},{8,9},{9,10},{10,1... | collective-permute-start | bytes 98312 | tf_op jit(solution)/shard_map/ppermute | solution.py:62
  23.9 5.1 %collective-permute-start.3 = (bf16[1,4,32,128]{3,2,1,0:T(8,128)(2,1)S(1)}, bf16[1,4,32,128]{3,2,1,0:T(8,128)(2,1)S(1)}, u32[]{:S(2)}, u32[]{:S(2)}) collective-permute-start(bf16[1,4,32,128]{3,2,1,0:T(8,128)(2,1)S(1)} %collective-permute-done.2), channel_id=1, source_target_pairs={{0,1},{1,2},{2,3},{3,4},{4,5},{5,6},{6,7},{7,0},{8,9},{9,10},{10,1... | collective-permute-start | bytes 98312 | tf_op jit(solution)/shard_map/ppermute | solution.py:62
  29.0 5.1 %collective-permute-start.4 = (bf16[1,4,32,128]{3,2,1,0:T(8,128)(2,1)S(1)}, bf16[1,4,32,128]{3,2,1,0:T(8,128)(2,1)S(1)}, u32[]{:S(2)}, u32[]{:S(2)}) collective-permute-start(bf16[1,4,32,128]{3,2,1,0:T(8,128)(2,1)S(1)} %collective-permute-done.3), channel_id=1, source_target_pairs={{0,1},{1,2},{2,3},{3,4},{4,5},{5,6},{6,7},{7,0},{8,9},{9,10},{10,1... | collective-permute-start | bytes 98312 | tf_op jit(solution)/shard_map/ppermute | solution.py:62
  34.1 5.1 %collective-permute-start.5 = (bf16[1,4,32,128]{3,2,1,0:T(8,128)(2,1)S(1)}, bf16[1,4,32,128]{3,2,1,0:T(8,128)(2,1)S(1)}, u32[]{:S(2)}, u32[]{:S(2)}) collective-permute-start(bf16[1,4,32,128]{3,2,1,0:T(8,128)(2,1)S(1)} %collective-permute-done.4), channel_id=1, source_target_pairs={{0,1},{1,2},{2,3},{3,4},{4,5},{5,6},{6,7},{7,0},{8,9},{9,10},{10,1... | collective-permute-start | bytes 98312 | tf_op jit(solution)/shard_map/ppermute | solution.py:62
  39.3 5.1 %collective-permute-start.6 = (bf16[1,4,32,128]{3,2,1,0:T(8,128)(2,1)S(1)}, bf16[1,4,32,128]{3,2,1,0:T(8,128)(2,1)S(1)}, u32[]{:S(2)}, u32[]{:S(2)}) collective-permute-start(bf16[1,4,32,128]{3,2,1,0:T(8,128)(2,1)S(1)} %collective-permute-done.5), channel_id=1, source_target_pairs={{0,1},{1,2},{2,3},{3,4},{4,5},{5,6},{6,7},{7,0},{8,9},{9,10},{10,1... | collective-permute-start | bytes 98312 | tf_op jit(solution)/shard_map/ppermute | solution.py:62
  47.1 1.6 copy-start.2
  48.7 56.9 %reduce-scatter.3.cloned.1.call-start = ((), (), s32[]{:S(2)}) async-start(), calls=%async_computation.2 | async-start | bytes 589824 | tf_op jit(solution)/shard_map/reduce_scatter | solution.py:54
  58.7 2.3 copy-start
  58.7 2.8 %copy-start.1 = (bf16[4,128,128]{2,1,0:T(8,128)(2,1)S(1)}, bf16[4,128,128]{2,1,0:T(8,128)(2,1)}, u32[]{:S(2)}) copy-start(bf16[4,128,128]{2,1,0:T(8,128)(2,1)} %param.13) | copy-start | bytes 393220
  58.7 2.9 %copy-start.3 = (f32[128]{0:T(128)S(1)}, f32[128]{0:T(128)}, u32[]{:S(2)}) copy-start(f32[128]{0:T(128)} %param.11) | copy-start | bytes 1540
  58.7 2.9 %copy-start.4 = (f32[128]{0:T(128)S(1)}, f32[128]{0:T(128)}, u32[]{:S(2)}) copy-start(f32[128]{0:T(128)} %param.12) | copy-start | bytes 1540
  60.9 175.7 %all-reduce.2.cloned.1.call-start = ((), (), s32[]{:S(2)}) async-start(), calls=%async_computation.4 | async-start | bytes 524288 | tf_op jit(solution)/shard_map/psum | solution.py:83
Sparse Core Ops, SparseCore 0:
  48.8 23.0 reduce-scatter.4
  74.2 31.3 reduce-scatter.2
  111.7 124.8 all-reduce.1
